TPU v7x, 32 devices: a whole 2x2x4 slice. The times are simulated.
32 devices in a mesh: tm: 8 (over z, x), tp: 4 (over y, core).
Axes of the slice: x: 2, y: 2, z: 4, core: 2. Of those that a mesh axis runs over, the one named last changes fastest.
Arguments:
- trajectory: float32 [16, 128, 3072], P('tm', None, 'tp'), may hold values from -6 to 6
- offset: int32 [1], replicated, may hold values from 0 to 15
- step_gaps: int32 [16], P('tm'), may hold values from 1 to 4, as said below
- qkv_weight: bfloat16 [3072, 3, 3072], P(None, None, 'tp')
- out_weight: bfloat16 [3072, 3072], P('tp'), may hold values from -4 to 4
- mod_weight: bfloat16 [256, 3, 3072], P(None, None, 'tp'), may hold values from -0.375 to 0.375
Outputs:
- advanced: float32 [16, 128, 3072], P('tm', None, 'tp')
Inputs may be any that keep to these rules, and one draw needn't show every extreme that they name: `step_gaps`: in aligned blocks of 2 timesteps, the gaps of block b sum to an even number for even b and to an odd number for odd b.
All inputs are finite; a program needn't handle non-finite values.
Results may differ from a plain program's by a relative error of at most 0.007.
Values may be sent and summed in bfloat16 or wider, within the bound.
A program may use at most 128 MiB of HBM per device.

v0:
```python
import math
import jax
import jax.numpy as jnp
from jax import lax
from jax.sharding import PartitionSpec as P

HD = 128
FREQ = 256
ITERS = 2


def prefix(array, axis, combine, identity):
    size, place = (lax.axis_size(axis), lax.axis_index(axis))
    everything = lax.all_gather(array, axis)
    start = jnp.broadcast_to(jnp.asarray(identity, array.dtype), array.shape)

    def turn(k, before):
        reached = k < place
        new = combine(before, everything[k])
        return jnp.where(reached, new, before)

    return lax.fori_loop(0, size, turn, start)


def prefix_2(array, axis, join, neutral):
    place = lax.axis_index(axis)
    gathered = lax.all_gather(array.astype(jnp.bfloat16), axis)
    state = jnp.zeros_like(array) + jnp.asarray(neutral, array.dtype)

    def one(turn, state):
        return join(state, lax.dynamic_index_in_dim(gathered, turn, 0, False).astype(array.dtype))

    return lax.fori_loop(0, place, one, state)


def add_up(earlier, later):
    return earlier + later


def embedding(sigma):
    half_freq = FREQ // 2
    frequencies = jnp.exp(-math.log(10000.0) * jnp.arange(half_freq, dtype=jnp.float32) / half_freq)
    angles = 1000.0 * sigma[:, None] * frequencies[None, :]
    return jnp.concatenate([jnp.cos(angles), jnp.sin(angles)], -1).astype(jnp.bfloat16)


def body(trajectory, offset, step_gaps, qkv_weight, out_weight, mod_weight):
    steps_here, tok_count, col_count = trajectory.shape
    full_width = qkv_weight.shape[0]
    time_count = steps_here * lax.axis_size("tm")
    level_count = 5 * time_count
    before = prefix(jnp.sum(step_gaps), "tm", add_up, jnp.int32(0))
    levels = (offset[0] + before + jnp.cumsum(step_gaps) - step_gaps).astype(jnp.float32)
    sigma = 1.0 - levels / level_count
    step_size = step_gaps.astype(jnp.float32) / level_count
    embed_rows = embedding(sigma)
    full_mod = lax.all_gather(mod_weight, "tp", axis=2, tiled=True)
    modulation = jnp.dot(
        embed_rows, full_mod.reshape(FREQ, 3 * full_width), preferred_element_type=jnp.float32
    ).reshape(steps_here, 3, full_width)
    gate_rows = lax.dynamic_slice_in_dim(
        modulation[:, 2], lax.axis_index("tp") * col_count, col_count, 1
    )
    first_point = jnp.where(lax.axis_index("tm") == 0, trajectory[0], jnp.zeros_like(trajectory[0]))
    flat_qkv = qkv_weight.reshape(full_width, -1)
    states = trajectory
    points = trajectory
    for sweep in range(ITERS):
        whole_rows = lax.all_gather(states, "tp", axis=2, tiled=True)
        row_mean = jnp.sum(whole_rows, -1, keepdims=True) / full_width
        variance = (
            jnp.sum(whole_rows * whole_rows, -1, keepdims=True) / full_width - row_mean * row_mean
        )
        inv_std = lax.rsqrt(variance + 1e-06)
        normed = (
            (whole_rows - row_mean) * inv_std * (1.0 + modulation[:, 1][:, None, :])
            + modulation[:, 0][:, None, :]
        ).astype(jnp.bfloat16)
        projected = jnp.einsum("std,de->ste", normed, flat_qkv, preferred_element_type=jnp.float32)
        projected = projected.astype(jnp.bfloat16).reshape(steps_here, tok_count, 3, -1, HD)
        queries = projected[:, :, 0]
        key_rows = projected[:, :, 1]
        values = projected[:, :, 2]
        scores = jnp.einsum(
            "sqhd,skhd->shqk", queries, key_rows, preferred_element_type=jnp.float32
        ) * (1.0 / math.sqrt(HD))
        row_max = jnp.max(scores, -1, keepdims=True)
        weights_exp = jnp.exp(scores - row_max)
        probs = (weights_exp / jnp.sum(weights_exp, -1, keepdims=True)).astype(jnp.bfloat16)
        attended = jnp.einsum(
            "shqk,skhd->sqhd", probs, values, preferred_element_type=jnp.float32
        ).astype(jnp.bfloat16)
        attended = attended.reshape(steps_here, tok_count, -1)
        head_out = jnp.einsum(
            "sqe,ed->sqd", attended, out_weight, preferred_element_type=jnp.float32
        )
        col_share = lax.psum_scatter(
            head_out.astype(jnp.bfloat16), "tp", scatter_dimension=2, tiled=True
        ).astype(jnp.float32)
        drifts = gate_rows[:, None, :] * col_share
        increments = -step_size[:, None, None] * drifts
        local_cum = jnp.cumsum(increments, 0)
        prefix_sum = prefix_2(
            local_cum[-1] + first_point,
            "tm",
            add_up,
            jnp.zeros((tok_count, col_count), jnp.float32),
        )
        entry_point = prefix_sum + first_point
        points = entry_point[None] + local_cum
        states = jnp.concatenate([entry_point[None], points[:-1]], 0)
    return points


def solution(mesh):
    placed = (
        P("tm", None, "tp"),
        P(),
        P("tm"),
        P(None, None, "tp"),
        P("tp", None),
        P(None, None, "tp"),
    )
    return jax.shard_map(
        body, mesh=mesh, in_specs=placed, out_specs=P("tm", None, "tp"), check_vma=False
    )
```

profile of v0, /device:TPU:26, one launch (start us, length us, event | category | flops | bytes accessed | tf_op | source)
XLA Modules:
  0.0 313.7 jit_solution(12103827058173000939)
XLA Ops:
  6.5 0.7 all-gather.8.cloned.1.call-update
  7.3 2.4 copy.33
  9.8 0.7 dynamic-slice.1
  10.5 0.6 reduce_sum.63
  11.1 1.4 dynamic-update-slice
  12.6 8.2 %all-reduce = s32[8]{0:T(128)S(1)} all-reduce(s32[8]{0:T(128)S(1)} %dynamic-update-slice), channel_id=1, replica_groups=mesh['tm'=8,'tp'=4] {'tm'}, use_global_device_ids=true, to_apply=%add | all-reduce | flops 8 | bytes 64
  21.4 0.2 reduce-window.9
  21.6 18.7 %copy.34 = bf16[3072,3,768]{0,2,1:T(8,128)(2,1)} copy(bf16[3072,3,768]{2,0,1:T(8,128)(2,1)} %param.15) | data formatting | bytes 28311552 | tf_op args[3]
  40.3 10.1 %while.33 = (s32[]{:T(128)}, s32[]{:T(128)}, s32[]{:T(128)}, s32[8]{0:T(128)S(1)}, s32[]{:T(128)}) while((s32[]{:T(128)}, s32[]{:T(128)}, s32[]{:T(128)}, s32[8]{0:T(128)S(1)}, s32[]{:T(128)}) %tuple.62), condition=%wide.region_2.3_spmd, body=%wide.region_1.2_spmd.sunk | while | flops 5 | bytes 107 | solution.py:22
  40.3 0.6 dynamic_slice.24
  41.6 0.6 dynamic_slice.24
  42.8 0.6 dynamic_slice.24
  44.1 0.6 dynamic_slice.24
  45.4 0.6 dynamic_slice.24
  46.6 0.6 dynamic_slice.24
  47.9 0.6 dynamic_slice.24
  49.2 0.6 dynamic_slice.24
  50.5 0.1 fusion.43
  50.6 2.4 fusion.57
  53.1 24.4 %all-gather.6.cloned.1.call-done = bf16[256,3,3072]{0,2,1:T(8,128)(2,1)} async-done(((bf16[256,3,768]{0,2,1:T(8,128)(2,1)}), bf16[256,3,3072]{0,2,1:T(8,128)(2,1)}) %all-gather.6.cloned.1.call-update) | async-done | bytes 4718608 | tf_op jit(solution)/shard_map/all_gather | solution.py:57
  77.4 3.6 %fusion.2 = f32[2,3,3072]{2,0,1:T(2,128)S(1)} fusion(bf16[256,3,3072]{0,2,1:T(8,128)(2,1)} %all-gather.6.cloned.1.call-done, bf16[2,128]{1,0:T(2,128)(2,1)S(1)} %get-tuple-element.169, bf16[2,128]{1,0:T(2,128)(2,1)S(1)} %get-tuple-element.168), kind=kOutput, calls=%fused_computation.4 | convolution fusion | flops 9439232 | bytes 4793344 | tf_op jit(solution)/shard_map/dot_general | solution.py:58
  81.1 10.0 %convolution_convert_fusion.1 = bf16[2,128,2304]{2,1,0:T(8,128)(2,1)S(1)} fusion(bf16[3072,2304,1]{0,1,2:T(8,128)(2,1)} %bitcast.117, f32[2,128,3072]{2,1,0:T(8,128)} %all-gather.8.cloned.1.call-done, f32[2,3072]{1,0:T(2,128)S(1)} %get-tuple-element.162, f32[2,3072]{1,0:T(2,128)S(1)} %get-tuple-element.163, f32[2,128]{1,0:T(2,128)S(1)} %get-tuple-element.167, ...), kind=kOutput, calls=%fused_computation.13 | convolution fusion | flops 3628400640 | bytes 18532352 | tf_op jit(solution)/shard_map/std,de->ste/dot_general | solution.py:79
  91.1 0.7 copy.36
  91.9 0.3 convolution_multiply_fusion.1
  92.2 0.4 fusion.59
  92.6 0.4 convolution_convert_fusion.3
  93.0 5.0 %fusion.8 = bf16[2,128,3072]{2,1,0:T(8,128)(2,1)} fusion(bf16[2,128,768]{1,2,0:T(8,128)(2,1)S(1)} %bitcast.126, bf16[768,3072]{1,0:T(8,128)(2,1)} %param.16), kind=kOutput, calls=%fused_computation.10 | convolution fusion | flops 1208745984 | bytes 6684672 | tf_op jit(solution)/shard_map/sqe,ed->sqd/dot_general | solution.py:94
  98.1 28.1 %reduce-scatter.3.cloned.1.call-done = bf16[2,128,768]{2,1,0:T(8,128)(2,1)} async-done(((bf16[2,128,3072]{2,1,0:T(8,128)(2,1)}), bf16[2,128,768]{2,1,0:T(8,128)(2,1)}) %reduce-scatter.3.cloned.1.call-update) | async-done | bytes 393232 | tf_op jit(solution)/shard_map/reduce_scatter | solution.py:97
  126.2 1.1 fusion.30
  127.3 0.7 fusion.35
  128.1 41.8 %all-gather.10.cloned.1.call-done = bf16[8,128,768]{2,1,0:T(8,128)(2,1)} async-done(((bf16[1,128,768]{2,1,0:T(8,128)(2,1)}), bf16[8,128,768]{2,1,0:T(8,128)(2,1)}) %all-gather.10.cloned.1.call-update) | async-done | bytes 1572880 | tf_op jit(solution)/shard_map/all_gather | solution.py:27
  169.9 7.2 %while.34 = (s32[]{:T(128)}, f32[128,768]{1,0:T(8,128)S(1)}, s32[]{:T(128)}, bf16[8,128,768]{2,1,0:T(8,128)(2,1)}, s32[]{:T(128)}, /*index=5*/s32[]{:T(128)}, s32[]{:T(128)}) while((s32[]{:T(128)}, f32[128,768]{1,0:T(8,128)S(1)}, s32[]{:T(128)}, bf16[8,128,768]{2,1,0:T(8,128)(2,1)}, s32[]{:T(128)}, /*index=5*/s32[]{:T(128)}, ...), condition=%wide.region_11.12_spmd, body=%wide.region_10.11_spmd.sunk | while | flops 196613 | bytes 983155 | solution.py:33
  170.0 1.0 convert_add_fusion.4
  171.0 1.0 convert_add_fusion.4
  172.0 1.0 convert_add_fusion.4
  173.1 1.0 convert_add_fusion.4
  174.1 1.0 convert_add_fusion.4
  175.1 1.0 convert_add_fusion.4
  176.1 1.0 convert_add_fusion.4
  177.2 0.1 slice_add_fusion.1
  177.3 0.9 pad_maximum_fusion
  178.2 0.2 reduce-scatter.5.cloned.1.call-start
  178.5 29.3 %all-gather.12.cloned.1.call-done = f32[2,128,3072]{2,1,0:T(8,128)} async-done(((f32[2,128,768]{2,1,0:T(8,128)}), f32[2,128,3072]{2,1,0:T(8,128)}) %all-gather.12.cloned.1.call-update) | async-done | bytes 3145744 | tf_op jit(solution)/shard_map/all_gather | solution.py:69
  207.8 2.6 fusion.56
  210.4 0.2 copy-done.1
  210.6 9.2 %convolution_convert_fusion = bf16[2,128,2304]{2,1,0:T(8,128)(2,1)S(1)} fusion(bf16[3072,2304,1]{0,1,2:T(8,128)(2,1)} %bitcast.118, f32[2,128,3072]{2,1,0:T(8,128)S(1)} %copy-done.1, f32[2,128]{1,0:T(2,128)S(1)} %get-tuple-element.165, f32[2,128]{1,0:T(2,128)S(1)} %get-tuple-element.164, f32[2,3072]{1,0:T(2,128)} %copy-done.2, f32[2,3072]{1,0:T(2,128)} %copy-done.3), kind=kOutput, calls=%fused_computation.12 | convolution fusion | flops 3628400640 | bytes 18532352 | tf_op jit(solution)/shard_map/std,de->ste/dot_general | solution.py:79
  219.8 0.7 copy.43
  220.5 0.3 convolution_multiply_fusion
  220.9 0.4 fusion.60
  221.3 0.4 convolution_convert_fusion.2
  221.7 4.9 %fusion.11 = bf16[2,128,3072]{2,1,0:T(8,128)(2,1)} fusion(bf16[2,128,768]{1,2,0:T(8,128)(2,1)S(1)} %bitcast.127, bf16[768,3072]{1,0:T(8,128)(2,1)} %param.16), kind=kOutput, calls=%fused_computation.11 | convolution fusion | flops 1208745984 | bytes 6684672 | tf_op jit(solution)/shard_map/sqe,ed->sqd/dot_general | solution.py:94
  226.6 28.1 %reduce-scatter.5.cloned.1.call-done = bf16[2,128,768]{2,1,0:T(8,128)(2,1)} async-done(((bf16[2,128,3072]{2,1,0:T(8,128)(2,1)}), bf16[2,128,768]{2,1,0:T(8,128)(2,1)}) %reduce-scatter.5.cloned.1.call-update) | async-done | bytes 393232 | tf_op jit(solution)/shard_map/reduce_scatter | solution.py:97
  254.8 1.1 fusion.26
  255.9 0.7 fusion.34
  256.6 42.0 %all-gather.14.cloned.1.call-done = bf16[8,128,768]{2,1,0:T(8,128)(2,1)} async-done(((bf16[1,128,768]{2,1,0:T(8,128)(2,1)}), bf16[8,128,768]{2,1,0:T(8,128)(2,1)}) %all-gather.14.cloned.1.call-update) | async-done | bytes 1572880 | tf_op jit(solution)/shard_map/all_gather | solution.py:27
  298.6 7.2 %while.35 = (s32[]{:T(128)}, f32[128,768]{1,0:T(8,128)S(1)}, s32[]{:T(128)}, bf16[8,128,768]{2,1,0:T(8,128)(2,1)}, s32[]{:T(128)}, /*index=5*/s32[]{:T(128)}, s32[]{:T(128)}) while((s32[]{:T(128)}, f32[128,768]{1,0:T(8,128)S(1)}, s32[]{:T(128)}, bf16[8,128,768]{2,1,0:T(8,128)(2,1)}, s32[]{:T(128)}, /*index=5*/s32[]{:T(128)}, ...), condition=%wide.region_19.20_spmd, body=%wide.region_18.19_spmd.sunk | while | flops 196613 | bytes 983155 | solution.py:33
  298.7 1.0 convert_add_fusion.5
  299.7 1.0 convert_add_fusion.5
  300.7 1.0 convert_add_fusion.5
  301.7 1.0 convert_add_fusion.5
  302.8 1.0 convert_add_fusion.5
  303.8 1.0 convert_add_fusion.5
  304.8 1.0 convert_add_fusion.5
  305.9 0.9 broadcast_add_fusion
  (35 shorter events, 0.6 us)
Async XLA Ops:
  6.5 3.3 %copy-start.5 = (u32[32]{0:T(128)S(1)}, u32[32]{0:T(128)}, u32[]{:S(2)}) copy-start(u32[32]{0:T(128)} %constant.91) | copy-start | bytes 388
  6.5 3.9 %copy-start.4 = (s32[2]{0:T(128)S(1)}, s32[2]{0:T(128)}, u32[]{:S(2)}) copy-start(s32[2]{0:T(128)} %param.14) | copy-start | bytes 28
  6.5 44.1 %all-gather.8.cloned.1.call-start = ((), (), s32[]{:S(2)}) async-start(), calls=%async_computation.3 | async-start | bytes 3932160 | tf_op jit(solution)/shard_map/all_gather | solution.py:69
  7.3 70.2 %all-gather.6.cloned.1.call-start = ((), (), s32[]{:S(2)}) async-start(), calls=%async_computation.2 | async-start | bytes 5898240 | tf_op jit(solution)/shard_map/all_gather | solution.py:57
  9.7 116.5 %reduce-scatter.3.cloned.1.call-start = ((), (), s32[]{:S(2)}) async-start(), calls=%async_computation.4 | async-start | bytes 1966080 | tf_op jit(solution)/shard_map/reduce_scatter | solution.py:97
  81.1 10.0 %copy-start.2 = (f32[2,3072]{1,0:T(2,128)}, f32[2,3072]{1,0:T(2,128)S(1)}, u32[]{:S(2)}) copy-start(f32[2,3072]{1,0:T(2,128)S(1)} %get-tuple-element.162) | copy-start | bytes 73732
  81.1 10.0 %copy-start.3 = (f32[2,3072]{1,0:T(2,128)}, f32[2,3072]{1,0:T(2,128)S(1)}, u32[]{:S(2)}) copy-start(f32[2,3072]{1,0:T(2,128)S(1)} %get-tuple-element.163) | copy-start | bytes 73732
  93.0 34.3 %copy-start = (f32[2,128,768]{2,1,0:T(8,128)S(1)}, f32[2,128,768]{2,1,0:T(8,128)}, u32[]{:S(2)}) copy-start(f32[2,128,768]{2,1,0:T(8,128)} %param.12) | copy-start | bytes 2359300
  98.0 71.9 %all-gather.10.cloned.1.call-start = ((), (), s32[]{:S(2)}) async-start(), calls=%async_computation.5 | async-start | bytes 1769472 | tf_op jit(solution)/shard_map/all_gather | solution.py:27
  128.1 79.7 %all-gather.12.cloned.1.call-start = ((), (), s32[]{:S(2)}) async-start(), calls=%async_computation.6 | async-start | bytes 3932160 | tf_op jit(solution)/shard_map/all_gather | solution.py:69
  178.2 76.5 %reduce-scatter.5.cloned.1.call-start = ((), (), s32[]{:S(2)}) async-start(), calls=%async_computation.7 | async-start | bytes 1966080 | tf_op jit(solution)/shard_map/reduce_scatter | solution.py:97
  207.8 2.8 copy-start.1
  226.6 72.0 %all-gather.14.cloned.1.call-start = ((), (), s32[]{:S(2)}) async-start(), calls=%async_computation.8 | async-start | bytes 1769472 | tf_op jit(solution)/shard_map/all_gather | solution.py:27
Sparse Core Ops, SparseCore 0:
  8.9 29.4 all-gather.7
  40.0 37.4 all-gather.5
  98.1 28.0 reduce-scatter.2
  128.3 41.6 all-gather.9
  178.3 29.4 all-gather.11
  226.7 28.0 reduce-scatter.4
  256.9 41.6 all-gather.13
where the time goes:
time: 315 us; the launch traced here: 314 us
  waiting for transfers between devices  195 us (62%)
  matrix products  34.9 us (11%)
  local copies, waits for them, and re-layouts  29.8 us (9%)
  other arithmetic  25.7 us (8%)
  between operations  14.4 us (5%)
  blocking collectives  8.23 us (3%)
  loops' own time  5.66 us (2%)
    all_gather x2, waiting for transfers between devices, prefix_2(): gathered = lax.all_gather(array.astype(jnp.bfloat16), axis)  83.7 us
    reduce_scatter x2, waiting for transfers between devices, body(): lax.psum_scatter(head_out.astype(jnp.bfloat16), 'tp', scatter_dimension=2...  56.3 us
    all_gather x2, waiting for transfers between devices, body(): whole_rows = lax.all_gather(states, 'tp', axis=2, tiled=True)  29.4 us
    all_gather x1, waiting for transfers between devices, body(): full_mod = lax.all_gather(mod_weight, 'tp', axis=2, tiled=True)  24.4 us
    unnamed x17, local copies, waits for them, and re-layouts  23.4 us
    dot_general x2, matrix products, body(): jnp.einsum('std,de->ste', normed, flat_qkv, preferred_element_type=jnp.fl...  19.1 us
    add x14, other arithmetic, add_up(): return earlier + later  14 us
    dot_general x2, matrix products, body(): jnp.einsum('sqe,ed->sqd', attended, out_weight, preferred_element_type=jn...  9.87 us
  transfers between devices with their start and end apart: 7, of which 6 were waited for; matrix products, arithmetic and copies ran while one was open for 10% of the time, Pallas kernels for 0%

commit v1 on v0

--- a/solution.py
+++ b/solution.py
@@ -1,3 +1,4 @@
+import functools
 import math
 import jax
 import jax.numpy as jnp
@@ -7,6 +8,24 @@
 HD = 128
 FREQ = 256
 ITERS = 2
+
+
+def keep_up_shards(local_array, row_axis, join_dim):
+    vals = []
+    parts_n = lax.axis_size(row_axis)
+    for j0 in range(1, parts_n):
+        vals.append((j0 - 1, j0))
+    z_new = vals + [(parts_n - 1, 0)]
+    finding = local_array
+    items = [finding]
+    for _ in range(parts_n - 1):
+        finding = lax.ppermute(finding, row_axis, z_new)
+        items += [finding]
+    met_up = jnp.concatenate([*reversed(items)], join_dim)
+    return jnp.roll(met_up, (lax.axis_index(row_axis) + 1) * finding.shape[join_dim], join_dim)
+
+
+wait_ways_here = functools.partial(keep_up_shards, row_axis="tp", join_dim=2)
 
 
 def prefix(array, axis, combine, identity):
@@ -54,7 +73,7 @@
     sigma = 1.0 - levels / level_count
     step_size = step_gaps.astype(jnp.float32) / level_count
     embed_rows = embedding(sigma)
-    full_mod = lax.all_gather(mod_weight, "tp", axis=2, tiled=True)
+    full_mod = wait_ways_here(mod_weight)
     modulation = jnp.dot(
         embed_rows, full_mod.reshape(FREQ, 3 * full_width), preferred_element_type=jnp.float32
     ).reshape(steps_here, 3, full_width)

time: 315 us -> 337 us (1.070)
  waiting for transfers between devices: 195 us -> 215 us
    ppermute x0 -> x3, waiting for transfers between devices: none -> 43.9 us  [keep_up_shards(): finding = lax.ppermute(finding, row_axis, z_new)]
    all_gather x1 -> x0, waiting for transfers between devices: 24.4 us -> none  [body(): full_mod = lax.all_gather(mod_weight, 'tp', axis=2, tiled=True)]
    unnamed x17 -> x28, local copies, waits for them, and re-layouts: 23.4 us -> 25.7 us
  transfers between devices with their start and end apart: 7 -> 9, of which waited for: 6 -> 7; matrix products, arithmetic and copies ran while one was open for 10% -> 9% of each run, Pallas kernels for 0% -> 0%
where the time goes in v1:
time: 337 us; the launch traced here: 336 us
  waiting for transfers between devices  215 us (64%)
  local copies, waits for them, and re-layouts  32.6 us (10%)
  matrix products  32.6 us (10%)
  other arithmetic  25.7 us (8%)
  between operations  14.5 us (4%)
  blocking collectives  8.23 us (2%)
  loops' own time  6.1 us (2%)
    all_gather x2, waiting for transfers between devices, prefix_2(): gathered = lax.all_gather(array.astype(jnp.bfloat16), axis)  83.8 us
    reduce_scatter x2, waiting for transfers between devices, body(): lax.psum_scatter(head_out.astype(jnp.bfloat16), 'tp', scatter_dimension=2...  57.5 us
    ppermute x3, waiting for transfers between devices, keep_up_shards(): finding = lax.ppermute(finding, row_axis, z_new)  43.9 us
    all_gather x2, waiting for transfers between devices, body(): whole_rows = lax.all_gather(states, 'tp', axis=2, tiled=True)  29.4 us
    unnamed x28, local copies, waits for them, and re-layouts  25.7 us
    dot_general x2, matrix products, body(): jnp.einsum('std,de->ste', normed, flat_qkv, preferred_element_type=jnp.fl...  19.1 us
    add x14, other arithmetic, add_up(): return earlier + later  14 us
    dot_general x2, matrix products, body(): jnp.einsum('sqe,ed->sqd', attended, out_weight, preferred_element_type=jn...  9.87 us
  transfers between devices with their start and end apart: 9, of which 7 were waited for; matrix products, arithmetic and copies ran while one was open for 9% of the time, Pallas kernels for 0%

profile of v1, /device:TPU:26, one launch (start us, length us, event | category | flops | bytes accessed | tf_op | source)
XLA Modules:
  0.0 335.9 jit_solution(13405608998375497594)
XLA Ops:
  6.5 1.6 copy.35
  8.3 23.1 %collective-permute-done = bf16[256,3,768]{0,2,1:T(8,128)(2,1)S(1)} collective-permute-done((bf16[256,3,768]{0,2,1:T(8,128)(2,1)S(1)}, bf16[256,3,768]{0,2,1:T(8,128)(2,1)S(1)}, u32[]{:S(2)}, u32[]{:S(2)}) %collective-permute-start) | collective-permute-done | bytes 1179680 | tf_op jit(solution)/shard_map/ppermute | solution.py:22
  31.4 1.1 collective-permute-start.1
  32.5 20.8 %collective-permute-done.1 = bf16[256,3,768]{0,2,1:T(8,128)(2,1)S(1)} collective-permute-done((bf16[256,3,768]{0,2,1:T(8,128)(2,1)S(1)}, bf16[256,3,768]{0,2,1:T(8,128)(2,1)S(1)}, u32[]{:S(2)}, u32[]{:S(2)}) %collective-permute-start.1) | collective-permute-done | bytes 1179680 | tf_op jit(solution)/shard_map/ppermute | solution.py:22
  53.3 0.7 dynamic-slice.1
  54.0 0.6 reduce_sum.63
  54.6 1.4 dynamic-update-slice
  56.1 8.2 %all-reduce = s32[8]{0:T(128)S(1)} all-reduce(s32[8]{0:T(128)S(1)} %dynamic-update-slice), channel_id=1, replica_groups=mesh['tm'=8,'tp'=4] {'tm'}, use_global_device_ids=true, to_apply=%add | all-reduce | flops 8 | bytes 64
  65.1 18.6 %copy.38 = bf16[3072,3,768]{0,2,1:T(8,128)(2,1)} copy(bf16[3072,3,768]{2,0,1:T(8,128)(2,1)} %param.15) | data formatting | bytes 28311552 | tf_op args[3]
  83.8 11.0 %while.33 = (s32[]{:T(128)}, s32[]{:T(128)}, s32[]{:T(128)}, s32[8]{0:T(128)S(1)}, s32[]{:T(128)}) while((s32[]{:T(128)}, s32[]{:T(128)}, s32[]{:T(128)}, s32[8]{0:T(128)S(1)}, s32[]{:T(128)}) %tuple.62), condition=%wide.region_2.3_spmd, body=%wide.region_1.2_spmd.sunk | while | flops 5 | bytes 107 | solution.py:41
  83.8 0.7 dynamic_slice.33
  85.1 0.7 dynamic_slice.33
  86.5 0.7 dynamic_slice.33
  87.9 0.7 dynamic_slice.33
  89.3 0.7 dynamic_slice.33
  90.7 0.7 dynamic_slice.33
  92.0 0.7 dynamic_slice.33
  93.4 0.7 dynamic_slice.33
  95.0 1.3 constant_dynamic-update-slice_fusion.7
  96.6 1.3 constant_dynamic-update-slice_fusion.3
  98.2 1.3 fusion.2
  99.6 2.6 fusion.59
  102.2 0.2 copy-done.1
  102.4 9.1 %convolution_convert_fusion.1 = bf16[2,128,2304]{2,1,0:T(8,128)(2,1)S(1)} fusion(bf16[3072,2304,1]{0,1,2:T(8,128)(2,1)} %bitcast.117, f32[2,128,3072]{2,1,0:T(8,128)S(1)} %copy-done.1, f32[2,3072]{1,0:T(2,128)S(1)} %get-tuple-element.162, f32[2,3072]{1,0:T(2,128)S(1)} %get-tuple-element.163, f32[2,128]{1,0:T(2,128)S(1)} %get-tuple-element.167, ...), kind=kOutput, calls=%fused_computation.14 | convolution fusion | flops 3628400640 | bytes 18532352 | tf_op jit(solution)/shard_map/std,de->ste/dot_general | solution.py:98
  111.6 0.7 copy.40
  112.3 0.3 convolution_multiply_fusion.1
  112.6 0.4 fusion.61
  113.1 0.4 convolution_convert_fusion.3
  113.5 5.0 %fusion.9 = bf16[2,128,3072]{2,1,0:T(8,128)(2,1)} fusion(bf16[2,128,768]{1,2,0:T(8,128)(2,1)S(1)} %bitcast.126, bf16[768,3072]{1,0:T(8,128)(2,1)} %param.16), kind=kOutput, calls=%fused_computation.11 | convolution fusion | flops 1208745984 | bytes 6684672 | tf_op jit(solution)/shard_map/sqe,ed->sqd/dot_general | solution.py:113
  118.5 29.4 %reduce-scatter.3.cloned.1.call-done = bf16[2,128,768]{2,1,0:T(8,128)(2,1)} async-done(((bf16[2,128,3072]{2,1,0:T(8,128)(2,1)}), bf16[2,128,768]{2,1,0:T(8,128)(2,1)}) %reduce-scatter.3.cloned.1.call-update) | async-done | bytes 393232 | tf_op jit(solution)/shard_map/reduce_scatter | solution.py:116
  147.9 1.1 fusion.31
  149.1 0.7 fusion.36
  149.9 41.9 %all-gather.7.cloned.1.call-done = bf16[8,128,768]{2,1,0:T(8,128)(2,1)} async-done(((bf16[1,128,768]{2,1,0:T(8,128)(2,1)}), bf16[8,128,768]{2,1,0:T(8,128)(2,1)}) %all-gather.7.cloned.1.call-update) | async-done | bytes 1572880 | tf_op jit(solution)/shard_map/all_gather | solution.py:46
  191.8 7.2 %while.34 = (s32[]{:T(128)}, f32[128,768]{1,0:T(8,128)S(1)}, s32[]{:T(128)}, bf16[8,128,768]{2,1,0:T(8,128)(2,1)}, s32[]{:T(128)}, /*index=5*/s32[]{:T(128)}, s32[]{:T(128)}) while((s32[]{:T(128)}, f32[128,768]{1,0:T(8,128)S(1)}, s32[]{:T(128)}, bf16[8,128,768]{2,1,0:T(8,128)(2,1)}, s32[]{:T(128)}, /*index=5*/s32[]{:T(128)}, ...), condition=%wide.region_11.12_spmd, body=%wide.region_10.11_spmd.sunk | while | flops 196613 | bytes 983155 | solution.py:52
  191.8 1.0 convert_add_fusion.4
  192.9 1.0 convert_add_fusion.4
  193.9 1.0 convert_add_fusion.4
  194.9 1.0 convert_add_fusion.4
  196.0 1.0 convert_add_fusion.4
  197.0 1.0 convert_add_fusion.4
  198.0 1.0 convert_add_fusion.4
  199.2 0.9 pad_maximum_fusion
  200.1 0.2 reduce-scatter.5.cloned.1.call-start
  200.3 29.3 %all-gather.9.cloned.1.call-done = f32[2,128,3072]{2,1,0:T(8,128)} async-done(((f32[2,128,768]{2,1,0:T(8,128)}), f32[2,128,3072]{2,1,0:T(8,128)}) %all-gather.9.cloned.1.call-update) | async-done | bytes 3145744 | tf_op jit(solution)/shard_map/all_gather | solution.py:88
  229.7 2.4 fusion.58
  232.2 10.0 %convolution_convert_fusion = bf16[2,128,2304]{2,1,0:T(8,128)(2,1)S(1)} fusion(bf16[3072,2304,1]{0,1,2:T(8,128)(2,1)} %bitcast.118, f32[2,128,3072]{2,1,0:T(8,128)} %all-gather.9.cloned.1.call-done, f32[2,128]{1,0:T(2,128)S(1)} %get-tuple-element.165, f32[2,128]{1,0:T(2,128)S(1)} %get-tuple-element.164, f32[2,3072]{1,0:T(2,128)S(1)} %copy-done.3, ...), kind=kOutput, calls=%fused_computation.13 | convolution fusion | flops 3628400640 | bytes 18532352 | tf_op jit(solution)/shard_map/std,de->ste/dot_general | solution.py:98
  242.2 0.7 copy.47
  242.9 0.3 convolution_multiply_fusion
  243.2 0.4 fusion.62
  243.7 0.4 convolution_convert_fusion.2
  244.0 4.9 %fusion.12 = bf16[2,128,3072]{2,1,0:T(8,128)(2,1)} fusion(bf16[2,128,768]{1,2,0:T(8,128)(2,1)S(1)} %bitcast.127, bf16[768,3072]{1,0:T(8,128)(2,1)} %param.16), kind=kOutput, calls=%fused_computation.12 | convolution fusion | flops 1208745984 | bytes 6684672 | tf_op jit(solution)/shard_map/sqe,ed->sqd/dot_general | solution.py:113
  249.0 28.1 %reduce-scatter.5.cloned.1.call-done = bf16[2,128,768]{2,1,0:T(8,128)(2,1)} async-done(((bf16[2,128,3072]{2,1,0:T(8,128)(2,1)}), bf16[2,128,768]{2,1,0:T(8,128)(2,1)}) %reduce-scatter.5.cloned.1.call-update) | async-done | bytes 393232 | tf_op jit(solution)/shard_map/reduce_scatter | solution.py:116
  277.1 1.1 fusion.27
  278.2 0.7 fusion.35
  279.0 41.8 %all-gather.11.cloned.1.call-done = bf16[8,128,768]{2,1,0:T(8,128)(2,1)} async-done(((bf16[1,128,768]{2,1,0:T(8,128)(2,1)}), bf16[8,128,768]{2,1,0:T(8,128)(2,1)}) %all-gather.11.cloned.1.call-update) | async-done | bytes 1572880 | tf_op jit(solution)/shard_map/all_gather | solution.py:46
  320.9 7.2 %while.35 = (s32[]{:T(128)}, f32[128,768]{1,0:T(8,128)S(1)}, s32[]{:T(128)}, bf16[8,128,768]{2,1,0:T(8,128)(2,1)}, s32[]{:T(128)}, /*index=5*/s32[]{:T(128)}, s32[]{:T(128)}) while((s32[]{:T(128)}, f32[128,768]{1,0:T(8,128)S(1)}, s32[]{:T(128)}, bf16[8,128,768]{2,1,0:T(8,128)(2,1)}, s32[]{:T(128)}, /*index=5*/s32[]{:T(128)}, ...), condition=%wide.region_19.20_spmd, body=%wide.region_18.19_spmd.sunk | while | flops 196613 | bytes 983155 | solution.py:52
  320.9 1.0 convert_add_fusion.5
  321.9 1.0 convert_add_fusion.5
  322.9 1.0 convert_add_fusion.5
  324.0 1.0 convert_add_fusion.5
  325.0 1.0 convert_add_fusion.5
  326.0 1.0 convert_add_fusion.5
  327.1 1.0 convert_add_fusion.5
  328.1 0.9 broadcast_add_fusion
  (50 shorter events, 1.4 us)
Async XLA Ops:
  6.5 46.8 %copy-start.7 = (u32[32]{0:T(128)S(1)}, u32[32]{0:T(128)}, u32[]{:S(2)}) copy-start(u32[32]{0:T(128)} %constant.110) | copy-start | bytes 388
  6.5 47.4 %copy-start.6 = (s32[2]{0:T(128)S(1)}, s32[2]{0:T(128)}, u32[]{:S(2)}) copy-start(s32[2]{0:T(128)} %param.14) | copy-start | bytes 28
  6.5 93.0 %all-gather.5.cloned.1.call-start = ((), (), s32[]{:S(2)}) async-start(), calls=%async_computation.2 | async-start | bytes 3932160 | tf_op jit(solution)/shard_map/all_gather | solution.py:88
  8.1 23.2 %collective-permute-start = (bf16[256,3,768]{0,2,1:T(8,128)(2,1)S(1)}, bf16[256,3,768]{0,2,1:T(8,128)(2,1)S(1)}, u32[]{:S(2)}, u32[]{:S(2)}) collective-permute-start(bf16[256,3,768]{0,2,1:T(8,128)(2,1)S(1)} %copy.35), channel_id=1, source_target_pairs={{0,1},{1,2},{2,3},{3,0},{4,5},{5,6},{6,7},{7,4},{8,9},{9,10},{10,1... | collective-permute-start | bytes 3538952 | tf_op jit(solution)/shard_map/ppermute | solution.py:22
  8.2 139.7 %reduce-scatter.3.cloned.1.call-start = ((), (), s32[]{:S(2)}) async-start(), calls=%async_computation.3 | async-start | bytes 1966080 | tf_op jit(solution)/shard_map/reduce_scatter | solution.py:116
  31.4 21.9 %collective-permute-start.1 = (bf16[256,3,768]{0,2,1:T(8,128)(2,1)S(1)}, bf16[256,3,768]{0,2,1:T(8,128)(2,1)S(1)}, u32[]{:S(2)}, u32[]{:S(2)}) collective-permute-start(bf16[256,3,768]{0,2,1:T(8,128)(2,1)S(1)} %collective-permute-done), channel_id=1, source_target_pairs={{0,1},{1,2},{2,3},{3,0},{4,5},{5,6},{6,7},{7,4},{8,9},{9,10},{10,1... | collective-permute-start | bytes 3538952 | tf_op jit(solution)/shard_map/ppermute | solution.py:22
  53.3 41.6 %collective-permute-start.2 = (bf16[256,3,768]{0,2,1:T(8,128)(2,1)S(1)}, bf16[256,3,768]{0,2,1:T(8,128)(2,1)}, u32[]{:S(2)}, u32[]{:S(2)}) collective-permute-start(bf16[256,3,768]{0,2,1:T(8,128)(2,1)S(1)} %collective-permute-done.1), channel_id=1, source_target_pairs={{0,1},{1,2},{2,3},{3,0},{4,5},{5,6},{6,7},{7,4},{8,9},{9,10},{10,1... | collective-permute-start | bytes 3538952 | tf_op jit(solution)/shard_map/ppermute | solution.py:22
  99.5 12.0 %copy-start.2 = (f32[2,3072]{1,0:T(2,128)}, f32[2,3072]{1,0:T(2,128)S(1)}, u32[]{:S(2)}) copy-start(f32[2,3072]{1,0:T(2,128)S(1)} %get-tuple-element.162) | copy-start | bytes 73732
  99.6 12.0 %copy-start.4 = (f32[2,3072]{1,0:T(2,128)}, f32[2,3072]{1,0:T(2,128)S(1)}, u32[]{:S(2)}) copy-start(f32[2,3072]{1,0:T(2,128)S(1)} %get-tuple-element.163) | copy-start | bytes 73732
  99.6 2.8 copy-start.1
  113.4 35.6 %copy-start = (f32[2,128,768]{2,1,0:T(8,128)S(1)}, f32[2,128,768]{2,1,0:T(8,128)}, u32[]{:S(2)}) copy-start(f32[2,128,768]{2,1,0:T(8,128)} %param.12) | copy-start | bytes 2359300
  118.4 73.3 %all-gather.7.cloned.1.call-start = ((), (), s32[]{:S(2)}) async-start(), calls=%async_computation.4 | async-start | bytes 1769472 | tf_op jit(solution)/shard_map/all_gather | solution.py:46
  149.8 79.9 %all-gather.9.cloned.1.call-start = ((), (), s32[]{:S(2)}) async-start(), calls=%async_computation.5 | async-start | bytes 3932160 | tf_op jit(solution)/shard_map/all_gather | solution.py:88
  199.1 33.1 %copy-start.3 = (f32[2,3072]{1,0:T(2,128)S(1)}, f32[2,3072]{1,0:T(2,128)}, u32[]{:S(2)}) copy-start(f32[2,3072]{1,0:T(2,128)} %copy-done.2) | copy-start | bytes 73732
  199.1 33.1 %copy-start.5 = (f32[2,3072]{1,0:T(2,128)S(1)}, f32[2,3072]{1,0:T(2,128)}, u32[]{:S(2)}) copy-start(f32[2,3072]{1,0:T(2,128)} %copy-done.4) | copy-start | bytes 73732
  200.1 77.0 %reduce-scatter.5.cloned.1.call-start = ((), (), s32[]{:S(2)}) async-start(), calls=%async_computation.6 | async-start | bytes 1966080 | tf_op jit(solution)/shard_map/reduce_scatter | solution.py:116
  249.0 71.9 %all-gather.11.cloned.1.call-start = ((), (), s32[]{:S(2)}) async-start(), calls=%async_computation.7 | async-start | bytes 1769472 | tf_op jit(solution)/shard_map/all_gather | solution.py:46
Sparse Core Ops, SparseCore 0:
  8.9 36.4 all-gather.4
  118.6 29.3 reduce-scatter.2
  150.1 41.6 all-gather.6
  200.2 29.4 all-gather.8
  249.1 27.9 reduce-scatter.4
  279.2 41.6 all-gather.10
